TPU v7x, 32 devices: a whole 2x2x4 slice. The times are simulated.
32 devices in a mesh: gx: 8 (over y, x, core), gy: 4 (over z).
Axes of the slice: x: 2, y: 2, z: 4, core: 2. Of those that a mesh axis runs over, the one named last changes fastest.
Arguments:
- field: float32 [65536, 512], P(('gx', 'gy')), may hold values from -6 to 6
Outputs:
- spectrum: float32 [65536, 512], P('gx', 'gy')
All inputs are finite; a program needn't handle non-finite values.
Results may differ from a plain program's by a relative error of at most 0.00007.
Values sent between devices are 32-bit elements; how exact they have to be, the bound alone decides.
A program may use at most 64 MiB of HBM per device.

v0:
```python
import math

import jax
import jax.numpy as jnp
from jax import lax
from jax.sharding import PartitionSpec as P

P_SIZE = 256
Q = 256


highest = lax.Precision.HIGHEST


def mat_dot(left, right):
    return jnp.dot(left, right, precision=highest, preferred_element_type=jnp.float32)


def finish(spec_real, spec_imag, frequency):
    length = P_SIZE * Q
    phases = math.pi / (2.0 * length) * frequency.astype(jnp.float32)
    factor = math.sqrt(2.0 / length)
    return factor * (
        jnp.cos(phases)[:, :, None] * spec_real + jnp.sin(phases)[:, :, None] * spec_imag
    )


def body(field):
    groups = lax.axis_size("gx")
    position = lax.axis_index("gx")
    length = P_SIZE * Q
    joined = lax.all_to_all(field, "gy", split_axis=1, concat_axis=0, tiled=True)
    row_count = joined.shape[0]
    col_width = joined.shape[1]
    half_rows = P_SIZE // (2 * groups)
    local_q = Q // groups
    local_p = P_SIZE // groups
    paired = joined.reshape(row_count // 2, 2, col_width)
    even_rows = paired[:, 0].reshape(half_rows, Q, col_width)
    odd_rows = jnp.flip(paired[:, 1].reshape(half_rows, Q, col_width), axis=1)
    low_half, high_half = (
        lax.all_to_all(even_rows, "gx", split_axis=1, concat_axis=0, tiled=True),
        lax.all_to_all(odd_rows, "gx", split_axis=1, concat_axis=0, tiled=True),
    )
    freq_first = jnp.arange(P_SIZE, dtype=jnp.int32)
    place_low = jnp.arange(P_SIZE // 2, dtype=jnp.int32)
    place_high = P_SIZE - 1 - place_low
    two_pi = 2.0 * math.pi
    low_phase = (
        two_pi / P_SIZE * (freq_first[:, None] * place_low[None, :] % P_SIZE).astype(jnp.float32)
    )
    high_phase = (
        two_pi / P_SIZE * (freq_first[:, None] * place_high[None, :] % P_SIZE).astype(jnp.float32)
    )
    flat_low = low_half.reshape(P_SIZE // 2, local_q * col_width)
    flat_high = high_half.reshape(P_SIZE // 2, local_q * col_width)
    cos_part = (
        mat_dot(jnp.cos(low_phase), flat_low) + mat_dot(jnp.cos(high_phase), flat_high)
    ).reshape(P_SIZE, local_q, col_width)
    sin_part = (
        mat_dot(jnp.sin(low_phase), flat_low) + mat_dot(jnp.sin(high_phase), flat_high)
    ).reshape(P_SIZE, local_q, col_width)
    part_imag = -sin_part
    second_place = position * local_q + jnp.arange(local_q, dtype=jnp.int32)
    turn_phase = (
        two_pi / length * (freq_first[:, None] * second_place[None, :] % length).astype(jnp.float32)
    )
    turn_cos = jnp.cos(turn_phase)[:, :, None]
    turn_sin = jnp.sin(turn_phase)[:, :, None]
    turned_real = cos_part * turn_cos + part_imag * turn_sin
    turned_imag = part_imag * turn_cos - cos_part * turn_sin
    moved_real, moved_imag = (
        lax.all_to_all(turned_real, "gx", split_axis=0, concat_axis=1, tiled=True),
        lax.all_to_all(turned_imag, "gx", split_axis=0, concat_axis=1, tiled=True),
    )
    second_index = jnp.arange(Q, dtype=jnp.int32)
    row_phase = two_pi / Q * (second_index[:, None] * second_index[None, :] % Q).astype(jnp.float32)
    row_cos = jnp.cos(row_phase)
    row_sin = jnp.sin(row_phase)
    spec_real = jnp.einsum("jb,kbc->jkc", row_cos, moved_real, precision=highest) + jnp.einsum(
        "jb,kbc->jkc", row_sin, moved_imag, precision=highest
    )
    spec_imag = jnp.einsum("jb,kbc->jkc", row_cos, moved_imag, precision=highest) - jnp.einsum(
        "jb,kbc->jkc", row_sin, moved_real, precision=highest
    )
    block_rows = lax.dynamic_slice_in_dim(freq_first, position * local_p, local_p, 0)
    frequency = block_rows[None, :] + P_SIZE * second_index[:, None]
    result = finish(spec_real, spec_imag, frequency)
    arrived = lax.all_to_all(result, "gx", split_axis=0, concat_axis=1, tiled=True)
    return arrived.reshape(local_q * P_SIZE, col_width)


def solution(mesh):
    in_specs = (P(("gx", "gy"), None),)
    out_specs = P("gx", "gy")
    return jax.shard_map(body, mesh=mesh, in_specs=in_specs, out_specs=out_specs, check_vma=False)
```

profile of v0, /device:TPU:1, one launch (start us, length us, event | category | flops | bytes accessed | tf_op | source)
XLA Modules:
  0.0 379.7 jit_solution(13258083812697321297)
XLA Ops:
  0.0 5.3 %copy.15 = f32[2048,512]{0,1:T(8,128)} copy(f32[2048,512]{1,0:T(8,128)} %param.1) | data formatting | bytes 8388608 | tf_op args[0]
  5.3 99.3 %all_to_all.97 = f32[2048,4,128]{0,2,1:T(8,128)} all-to-all(f32[2048,4,128]{0,2,1:T(8,128)} %bitcast.81), channel_id=1, replica_groups=mesh['gx'=8,'gy'=4] {'gy'}, dimensions={1} | all-to-all | bytes 8388608 | tf_op jit(solution)/shard_map/all_to_all | solution.py:32
  104.7 5.3 %copy.16 = f32[4,2048,128]{2,1,0:T(8,128)} copy(f32[4,2048,128]{1,2,0:T(8,128)} %bitcast.79) | data formatting | bytes 8388608 | tf_op jit(solution)/shard_map/all_to_all | solution.py:32
  110.0 7.7 %fusion.96 = (f32[4096,1,128]{2,1,0:T(1,128)}, f32[4096,1,128]{2,1,0:T(1,128)S(1)}) fusion(f32[4096,2,128]{2,1,0:T(2,128)} %bitcast.78), kind=kLoop, calls=%fused_computation.111 | loop fusion | bytes 8388608 | tf_op jit(solution)/shard_map/slice | solution.py:40
  117.7 2.5 copy.17
  120.2 5.0 %all-to-all-start.1 = ((f32[16,256,128]{2,0,1:T(8,128)}), f32[16,256,128]{2,0,1:T(8,128)S(1)}, u32[]{:S(2)}, u32[]{:S(2)}) async-start(f32[16,256,128]{2,0,1:T(8,128)} %copy.17), calls=%async_computation.1 | async-start | bytes 4194304 | tf_op jit(solution)/shard_map/all_to_all | solution.py:42
  125.2 4.1 %copy.20 = f32[16,256,128]{2,0,1:T(8,128)} copy(f32[16,256,128]{2,1,0:T(8,128)} %bitcast.83) | data formatting | bytes 4194304 | tf_op jit(solution)/shard_map/reshape;squeeze | solution.py:40
  129.3 3.1 rev.4
  132.4 16.0 %all-to-all-done.1 = f32[16,256,128]{2,0,1:T(8,128)S(1)} async-done(((f32[16,256,128]{2,0,1:T(8,128)}), f32[16,256,128]{2,0,1:T(8,128)S(1)}, u32[]{:S(2)}, u32[]{:S(2)}) %all-to-all-start.1) | async-done | bytes 2097184 | tf_op jit(solution)/shard_map/all_to_all | solution.py:42
  148.4 8.2 %all-to-all-start.2 = ((f32[16,256,128]{2,0,1:T(8,128)}), f32[16,256,128]{2,0,1:T(8,128)}, u32[]{:S(2)}, u32[]{:S(2)}) async-start(f32[16,256,128]{2,0,1:T(8,128)} %rev.4), calls=%async_computation.2 | async-start | bytes 4194304 | tf_op jit(solution)/shard_map/all_to_all | solution.py:43
  156.7 0.5 fusion.57
  157.2 0.6 copy.19
  157.8 7.3 %fusion.9 = f32[256,4096]{1,0:T(8,128)} fusion(f32[16,8,32,128]{3,2,1,0:T(8,128)S(1)} %bitcast.73), kind=kOutput, calls=%fused_computation.16 | convolution fusion | flops 1611071488 | bytes 6291456 | tf_op jit(solution)/shard_map/dot_general | solution.py:16
  165.2 7.5 %fusion.7 = f32[256,4096]{1,0:T(8,128)} fusion(f32[16,8,32,128]{3,2,1,0:T(8,128)S(1)} %bitcast.74), kind=kOutput, calls=%fused_computation.14 | convolution fusion | flops 1611071488 | bytes 6291456 | tf_op jit(solution)/shard_map/dot_general | solution.py:16
  172.6 7.1 %all-to-all-done.2 = f32[16,256,128]{2,0,1:T(8,128)} async-done(((f32[16,256,128]{2,0,1:T(8,128)}), f32[16,256,128]{2,0,1:T(8,128)}, u32[]{:S(2)}, u32[]{:S(2)}) %all-to-all-start.2) | async-done | bytes 2097184 | tf_op jit(solution)/shard_map/all_to_all | solution.py:43
  179.7 0.0 copy-start.3
  179.7 2.4 copy.22
  182.1 0.4 copy-done.3
  182.6 4.9 %fusion.3 = f32[32,8,32,128]{3,1,2,0:T(8,128)S(1)} fusion(f32[256,4096]{1,0:T(8,128)S(1)} %copy-done.3, f32[16,8,32,128]{3,2,1,0:T(8,128)S(1)} %bitcast.75, s32[128]{0:T(128)S(1)} %iota_subtract_fusion), kind=kOutput, calls=%fused_computation.10 | convolution fusion | flops 1612120064 | bytes 10486272 | tf_op jit(solution)/shard_map/dot_general | solution.py:16
  187.5 0.0 copy-start.2
  187.5 0.8 copy.31
  188.3 1.4 copy-done.2
  189.7 5.0 %fusion.4 = f32[32,8,32,128]{3,1,2,0:T(8,128)S(1)} fusion(f32[256,4096]{1,0:T(8,128)S(1)} %copy-done.2, f32[16,8,32,128]{3,2,1,0:T(8,128)S(1)} %bitcast.76, s32[128]{0:T(128)S(1)} %iota_subtract_fusion), kind=kOutput, calls=%fused_computation.11 | convolution fusion | flops 1613168640 | bytes 10486272 | tf_op jit(solution)/shard_map/dot_general | solution.py:16
  194.7 1.0 copy.32
  195.6 4.6 %fusion.1 = (f32[256,32,128]{2,1,0:T(8,128)}, f32[256,32,128]{2,1,0:T(8,128)S(1)}) fusion(f32[32,8,32,128]{3,2,1,0:T(8,128)S(1)} %copy.32, f32[32,8,32,128]{3,2,1,0:T(8,128)S(1)} %copy.31, f32[256,32]{1,0:T(8,128)S(1)} %get-tuple-element.12, f32[256,32]{1,0:T(8,128)S(1)} %get-tuple-element.11), kind=kLoop, calls=%fused_computation.5 | loop fusion | flops 6291456 | bytes 16842752 | tf_op jit(solution)/shard_map/add | solution.py:70
  200.2 54.6 %all_to_all.98 = f32[256,32,128]{2,1,0:T(8,128)} all-to-all(f32[256,32,128]{2,1,0:T(8,128)S(1)} %get-tuple-element.6), channel_id=1, replica_groups=mesh['gx'=8,'gy'=4] {'gx'}, dimensions={0} | all-to-all | bytes 8388608 | tf_op jit(solution)/shard_map/all_to_all | solution.py:74
  254.9 5.7 %all-to-all-start.3 = ((f32[256,32,128]{2,1,0:T(8,128)}), f32[256,32,128]{2,1,0:T(8,128)}, u32[]{:S(2)}, u32[]{:S(2)}) async-start(f32[256,32,128]{2,1,0:T(8,128)} %get-tuple-element.5), calls=%async_computation.3 | async-start | bytes 8388608 | tf_op jit(solution)/shard_map/all_to_all | solution.py:73
  260.6 0.1 dynamic_slice.3
  260.6 0.2 fusion.63
  260.8 2.8 copy.24
  263.7 7.1 %fusion.19 = f32[256,32,128]{2,0,1:T(8,128)} fusion(f32[32,256,128]{2,1,0:T(8,128)S(1)} %bitcast.71), kind=kOutput, calls=%fused_computation.29 | convolution fusion | flops 3222142976 | bytes 8388608 | tf_op jit(solution)/shard_map/jb,kbc->jkc/dot_general | solution.py:80
  270.8 7.3 %fusion.21 = f32[256,32,128]{2,0,1:T(8,128)} fusion(f32[32,256,128]{2,1,0:T(8,128)S(1)} %bitcast.72), kind=kOutput, calls=%fused_computation.31 | convolution fusion | flops 3222142976 | bytes 8388608 | tf_op jit(solution)/shard_map/jb,kbc->jkc/dot_general | solution.py:83
  278.1 28.1 %all-to-all-done.3 = f32[256,32,128]{2,1,0:T(8,128)} async-done(((f32[256,32,128]{2,1,0:T(8,128)}), f32[256,32,128]{2,1,0:T(8,128)}, u32[]{:S(2)}, u32[]{:S(2)}) %all-to-all-start.3) | async-done | bytes 4194336 | tf_op jit(solution)/shard_map/all_to_all | solution.py:73
  306.2 2.8 copy.23
  309.0 0.0 copy-start
  309.0 0.0 copy-start.1
  309.0 4.8 %fusion.23 = f32[256,32,128]{2,0,1:T(8,128)S(1)} fusion(f32[32,256,128]{2,1,0:T(8,128)S(1)} %bitcast.69), kind=kOutput, calls=%fused_computation.33 | convolution fusion | flops 3222142976 | bytes 8388608 | tf_op jit(solution)/shard_map/jb,kbc->jkc/dot_general | solution.py:80
  313.8 0.0 copy-done
  313.8 0.0 copy-done.1
  313.8 6.1 %add_multiply_fusion = f32[256,32,128]{2,0,1:T(8,128)S(1)} fusion(f32[256,32,128]{2,0,1:T(8,128)S(1)} %copy-done.1, f32[256,32,128]{2,0,1:T(8,128)S(1)} %fusion.23, f32[256,32,128]{2,0,1:T(8,128)S(1)} %copy-done, f32[32,256,128]{2,1,0:T(8,128)S(1)} %bitcast.70, f32[256,32]{0,1:T(8,128)S(1)} %get-tuple-element.10, f32[256,32]{0,1:T(8,128)S(1)} %get-tuple-element.9), kind=kOutput, calls=%fused_computation.9 | convolution fusion | flops 3228434432 | bytes 21037056 | tf_op jit(solution)/shard_map/jb,kbc->jkc/dot_general | solution.py:83
  319.9 2.7 copy.25
  322.7 53.9 %all_to_all.99 = f32[256,32,128]{2,1,0:T(8,128)S(1)} all-to-all(f32[256,32,128]{2,1,0:T(8,128)S(1)} %copy.25), channel_id=1, replica_groups=mesh['gx'=8,'gy'=4] {'gx'}, dimensions={0} | all-to-all | bytes 8388608 | tf_op jit(solution)/shard_map/all_to_all | solution.py:89
  376.6 2.7 copy.26
  (4 shorter events, 0.0 us)
Async XLA Ops:
  120.2 28.2 %all-to-all-start.1 = ((f32[16,256,128]{2,0,1:T(8,128)}), f32[16,256,128]{2,0,1:T(8,128)S(1)}, u32[]{:S(2)}, u32[]{:S(2)}) async-start(f32[16,256,128]{2,0,1:T(8,128)} %copy.17), calls=%async_computation.1 | async-start | bytes 4194304 | tf_op jit(solution)/shard_map/all_to_all | solution.py:42
  148.4 31.3 %all-to-all-start.2 = ((f32[16,256,128]{2,0,1:T(8,128)}), f32[16,256,128]{2,0,1:T(8,128)}, u32[]{:S(2)}, u32[]{:S(2)}) async-start(f32[16,256,128]{2,0,1:T(8,128)} %rev.4), calls=%async_computation.2 | async-start | bytes 4194304 | tf_op jit(solution)/shard_map/all_to_all | solution.py:43
  179.7 2.8 copy-start.3
  187.5 2.2 copy-start.2
  254.9 51.3 %all-to-all-start.3 = ((f32[256,32,128]{2,1,0:T(8,128)}), f32[256,32,128]{2,1,0:T(8,128)}, u32[]{:S(2)}, u32[]{:S(2)}) async-start(f32[256,32,128]{2,1,0:T(8,128)} %get-tuple-element.5), calls=%async_computation.3 | async-start | bytes 8388608 | tf_op jit(solution)/shard_map/all_to_all | solution.py:73
  309.0 4.8 %copy-start = (f32[256,32,128]{2,0,1:T(8,128)S(1)}, f32[256,32,128]{2,0,1:T(8,128)}, u32[]{:S(2)}) copy-start(f32[256,32,128]{2,0,1:T(8,128)} %fusion.19) | copy-start | bytes 12582916
  309.0 4.8 %copy-start.1 = (f32[256,32,128]{2,0,1:T(8,128)S(1)}, f32[256,32,128]{2,0,1:T(8,128)}, u32[]{:S(2)}) copy-start(f32[256,32,128]{2,0,1:T(8,128)} %fusion.21) | copy-start | bytes 12582916
where the time goes:
time: 386 us; the launch traced here: 380 us
  blocking collectives  208 us (54%)
  waiting for transfers between devices  51.2 us (13%)
  matrix products  50 us (13%)
  local copies, waits for them, and re-layouts  45.8 us (12%)
  starting transfers between devices  18.9 us (5%)
  other arithmetic  5.36 us (1%)
    all_to_all x1, blocking collectives, body(): lax.all_to_all(field, 'gy', split_axis=1, concat_axis=0, tiled=True)  99.3 us
    all_to_all x1, blocking collectives, body(): lax.all_to_all(turned_imag, 'gx', split_axis=0, concat_axis=1, tiled=True)  54.6 us
    all_to_all x1, blocking collectives, body(): lax.all_to_all(result, 'gx', split_axis=0, concat_axis=1, tiled=True)  53.9 us
    all_to_all x1, waiting for transfers between devices, body(): lax.all_to_all(turned_real, 'gx', split_axis=0, concat_axis=1, tiled=True)  28.1 us
    dot_general x4, matrix products, mat_dot(): jnp.dot(left, right, precision=highest, preferred_element_type=jnp.float32)  24.7 us
    all_to_all x1, waiting for transfers between devices, body(): lax.all_to_all(even_rows, 'gx', split_axis=1, concat_axis=0, tiled=True)  16 us
    unnamed x11, local copies, waits for them, and re-layouts  8.93 us
    all_to_all x1, starting transfers between devices, body(): lax.all_to_all(odd_rows, 'gx', split_axis=1, concat_axis=0, tiled=True)  8.22 us
  transfers between devices with their start and end apart: 3, of which 3 were waited for; matrix products, arithmetic and copies ran while one was open for 11% of the time, Pallas kernels for 0%

commit v1 on v0

--- a/solution.py
+++ b/solution.py
@@ -1,14 +1,21 @@
+import functools
 import math
 
 import jax
 import jax.numpy as jnp
+import numpy as np
 from jax import lax
+from jax.experimental import pallas as pl
+from jax.experimental.pallas import tpu as pltpu
 from jax.sharding import PartitionSpec as P
 
 P_SIZE = 256
 Q = 256
-
-
+HALF = P_SIZE // 2
+LANES = 128
+STEP = 4
+
+MESH = pl.DeviceIdType.MESH
 highest = lax.Precision.HIGHEST
 
 
@@ -90,7 +97,289 @@
     return arrived.reshape(local_q * P_SIZE, col_width)
 
 
+def split_np(table):
+    high = table.astype(jnp.bfloat16)
+    low = (table - high.astype(np.float64)).astype(jnp.bfloat16)
+    return np.stack([high, low])
+
+
+def order_of_q(groups):
+    pairs = HALF // groups
+    order = []
+    for group in range(groups):
+        for start in range(0, pairs, STEP):
+            low = [group * pairs + start + i for i in range(STEP)]
+            order += low + [Q - 1 - q for q in low]
+    return np.array(order)
+
+
+def first_matrix():
+    low = np.arange(HALF)
+    place = np.concatenate([low, P_SIZE - 1 - low])
+    angle = 2 * np.pi / P_SIZE * (low[:, None] * place[None, :] % P_SIZE)
+    real, imag = np.cos(angle), -np.sin(angle)
+    imag[0] = np.cos(np.pi * place)
+    return split_np(np.concatenate([real, imag]))
+
+
+def second_matrices(groups):
+    length = P_SIZE * Q
+    q = order_of_q(groups)[None, :]
+    k2 = np.arange(Q)[:, None]
+    angle = 2 * np.pi / Q * (k2 * q % Q)
+    usual = np.concatenate([np.cos(angle), np.sin(angle)])
+    factor = math.sqrt(2.0 / length)
+    def row(k):
+        return factor * np.cos(2 * np.pi / (4 * length) * (k * (4 * q + 1) % (4 * length)))
+    special = np.concatenate([row(P_SIZE * k2), row(HALF + P_SIZE * (Q - 1 - k2))])
+    return np.stack([split_np(usual), split_np(special)])
+
+
+def split(value):
+    high = value.astype(jnp.bfloat16)
+    low = (value - high.astype(jnp.float32)).astype(jnp.bfloat16)
+    return high, low
+
+
+def three_dots(high, low, value):
+    value_high, value_low = split(value)
+    dot = functools.partial(jnp.dot, preferred_element_type=jnp.float32)
+    return dot(high, value_high) + (dot(high, value_low) + dot(low, value_high))
+
+
+def kernel(
+    groups, planes, x_ref, first_ref, second_ref, out_ref,
+    got_rows, part, got_part, coef, turn_cos, turn_sin, end_cos, end_sin,
+    recv_rows, send_rows, recv_part, send_part, recv_coef, send_coef,
+):
+    gx, gy = lax.axis_index("gx"), lax.axis_index("gy")
+    devices = groups * planes
+    length = P_SIZE * Q
+    pairs = HALF // groups
+    chunks = pairs // STEP
+    own = x_ref.shape[0]
+    width = 2 * STEP
+    block = Q // groups
+
+    barrier = pltpu.get_barrier_semaphore()
+
+    def target(offset):
+        return lax.rem(gx + offset // planes, groups), lax.rem(gy + offset % planes, planes)
+
+    def greet(offset, carry):
+        pl.semaphore_signal(barrier, inc=1, device_id=target(offset), device_id_type=MESH)
+        return carry
+
+    lax.fori_loop(1, devices, greet, 0)
+    pl.semaphore_wait(barrier, devices - 1)
+
+    first_place = (gx * planes + gy) * own
+
+    def row_copies(chunk, gxd, gyd):
+        low = pl.multiple_of((gxd * pairs + chunk * STEP) * 2, width)
+        high = pl.multiple_of(2 * Q - (gxd * pairs + (chunk + 1) * STEP) * 2, width)
+        columns = pl.ds(pl.multiple_of(gyd * LANES, LANES), LANES)
+        for side, at in ((0, low), (1, high)):
+            yield (
+                x_ref.at[:, pl.ds(at, width), columns],
+                got_rows.at[chunk, pl.ds(first_place, own), pl.ds(side * width, width), :],
+            )
+
+    def send_chunk(chunk, carry):
+        for source, place in row_copies(chunk, gx, gy):
+            pltpu.make_async_copy(source, place, recv_rows.at[chunk]).start()
+
+        def send(offset, carry):
+            gxd, gyd = target(offset)
+            for source, place in row_copies(chunk, gxd, gyd):
+                pltpu.make_async_remote_copy(
+                    src_ref=source, dst_ref=place, send_sem=send_rows,
+                    recv_sem=recv_rows.at[chunk], device_id=(gxd, gyd), device_id_type=MESH,
+                ).start()
+            return carry
+
+        lax.fori_loop(1, devices, send, 0)
+        return carry
+
+    lax.fori_loop(0, chunks, send_chunk, 0)
+
+    slot_row = lax.broadcasted_iota(jnp.int32, (HALF, LANES), 0)
+
+    def turn_table(at, carry):
+        chunk, inner = at // width, at % width
+        base = gx * pairs + chunk * STEP
+        q = jnp.where(inner < STEP, base + inner, Q - 1 - (base + inner - STEP))
+        angle = (slot_row * q).astype(jnp.float32) * (2 * math.pi / length)
+        turn_cos[at] = jnp.cos(angle)
+        turn_sin[at] = jnp.sin(angle)
+        return carry
+
+    lax.fori_loop(0, 2 * pairs, turn_table, 0)
+    k2_row = lax.broadcasted_iota(jnp.int32, (Q, LANES), 0)
+    end_angle = k2_row.astype(jnp.float32) * (math.pi * P_SIZE / (2 * length))
+    factor = math.sqrt(2.0 / length)
+    end_cos[...] = factor * jnp.cos(end_angle)
+    end_sin[...] = factor * jnp.sin(end_angle)
+
+    def first_stage(chunk, carry):
+        rows = got_rows.at[chunk]
+        pltpu.make_async_copy(rows, rows, recv_rows.at[chunk]).wait()
+        flat = rows.reshape(HALF * 2 * width, LANES)
+
+        def line(row):
+            return flat[pl.ds(row, HALF, stride=2 * width), :]
+
+        for i in range(STEP):
+            mirror = width + 2 * (STEP - 1 - i)
+            value = jnp.concatenate(
+                [
+                    jnp.concatenate([line(2 * i), line(mirror)], axis=1),
+                    jnp.concatenate([line(mirror + 1), line(2 * i + 1)], axis=1),
+                ],
+                axis=0,
+            )
+            both = three_dots(first_ref[0], first_ref[1], value)
+            for side in range(2):
+                inner = side * STEP + i
+                real = both[:HALF, side * LANES : (side + 1) * LANES]
+                imag = both[HALF:, side * LANES : (side + 1) * LANES]
+                cos = turn_cos[chunk * width + inner]
+                sin = turn_sin[chunk * width + inner]
+                turned = real * cos + imag * sin, imag * cos - real * sin
+                for plane in range(2):
+                    part[chunk, :, inner, plane] = turned[plane].reshape(groups, pairs, LANES)
+
+        pltpu.make_async_copy(part.at[chunk, gx], got_part.at[gx, chunk], recv_part).start()
+        for offset in range(1, groups):
+            other = lax.rem(gx + offset, groups)
+            pltpu.make_async_remote_copy(
+                src_ref=part.at[chunk, other], dst_ref=got_part.at[gx, chunk],
+                send_sem=send_part, recv_sem=recv_part,
+                device_id=(other, gy), device_id_type=MESH,
+            ).start()
+        return carry
+
+    lax.fori_loop(0, chunks, first_stage, 0)
+    pltpu.make_async_copy(got_part, got_part, recv_part).wait()
+
+    flat_part = got_part.reshape(Q * 2 * pairs, LANES)
+    flat_coef = coef.reshape(2 * Q * pairs, LANES)
+    eight = 8
+
+    def second_stage(slot, carry):
+        value = jnp.concatenate(
+            [
+                flat_part[pl.ds(plane * pairs + slot, Q, stride=2 * pairs), :]
+                for plane in range(2)
+            ],
+            axis=1,
+        )
+        frequency = gx * pairs + slot
+        alone = frequency == 0
+        which = jnp.where(alone, 1, 0)
+        product = three_dots(second_ref[which, 0], second_ref[which, 1], value)
+        top_real, top_imag = product[:Q, :LANES], product[:Q, LANES:]
+        low_real, low_imag = product[Q:, :LANES], product[Q:, LANES:]
+        spec_real = top_real + low_imag
+        spec_imag = top_imag - low_real
+        angle = jnp.full((8, LANES), frequency, jnp.int32).astype(jnp.float32) * (
+            math.pi / (2 * length)
+        )
+        cos_one, sin_one = jnp.cos(angle)[:1], jnp.sin(angle)[:1]
+        cos = end_cos[...] * cos_one - end_sin[...] * sin_one
+        sin = end_sin[...] * cos_one + end_cos[...] * sin_one
+        near = jnp.where(alone, top_real, cos * spec_real + sin * spec_imag)
+        far = jnp.where(alone, low_imag, sin * spec_real - cos * spec_imag)
+        flat_coef[pl.ds(slot, Q, stride=pairs), :] = near
+        flat_coef[pl.ds(Q * pairs + pairs - 1 - slot, Q, stride=pairs), :] = far
+        return carry
+
+    def coef_copies(step, other):
+        near = step * eight
+        far = pairs - eight - near
+        yield (
+            coef.at[0, pl.ds(pl.multiple_of(other * block, block), block), pl.ds(near, eight)],
+            out_ref.at[0, :, pl.ds(pl.multiple_of(gx * pairs + near, eight), eight)],
+        )
+        away = groups - 1 - other
+        yield (
+            coef.at[1, pl.ds(pl.multiple_of(away * block, block), block), pl.ds(far, eight)],
+            out_ref.at[1, :, pl.ds(pl.multiple_of((groups - 1 - gx) * pairs + far, eight), eight)],
+        )
+
+    for step in range(pairs // eight):
+        lax.fori_loop(step * eight, (step + 1) * eight, second_stage, 0)
+        for source, place in coef_copies(step, gx):
+            pltpu.make_async_copy(source, place, recv_coef).start()
+        for offset in range(1, groups):
+            other = lax.rem(gx + offset, groups)
+            for source, place in coef_copies(step, other):
+                pltpu.make_async_remote_copy(
+                    src_ref=source, dst_ref=place, send_sem=send_coef, recv_sem=recv_coef,
+                    device_id=(other, gy), device_id_type=MESH,
+                ).start()
+
+    pltpu.make_async_copy(out_ref, out_ref, recv_coef).wait()
+    sent = x_ref.at[:, pl.ds(0, 2 * Q - 2 * Q // devices), :]
+    pltpu.make_async_copy(sent, sent, send_rows).wait()
+    sent = part.at[:, pl.ds(0, groups - 1)]
+    pltpu.make_async_copy(sent, sent, send_part).wait()
+    sent = coef.at[:, pl.ds(0, Q - block)]
+    pltpu.make_async_copy(sent, sent, send_coef).wait()
+
+
+def fused_body(field):
+    groups, planes = lax.axis_size("gx"), lax.axis_size("gy")
+    pairs = HALF // groups
+    chunks = pairs // STEP
+    block = Q // groups
+    own = field.shape[0] // (2 * Q)
+    width = 2 * STEP
+    f32 = jnp.float32
+    vmem = pl.BlockSpec(memory_space=pltpu.VMEM)
+    dma = pltpu.SemaphoreType.DMA
+    both = pl.pallas_call(
+        functools.partial(kernel, groups, planes),
+        out_shape=jax.ShapeDtypeStruct((2, block, HALF, LANES), f32),
+        in_specs=[pl.BlockSpec(memory_space=pl.ANY), vmem, vmem],
+        out_specs=vmem,
+        scratch_shapes=[
+            pltpu.VMEM((chunks, HALF, 2 * width, LANES), f32),
+            pltpu.VMEM((chunks, groups, width, 2, pairs, LANES), f32),
+            pltpu.VMEM((groups, chunks, width, 2, pairs, LANES), f32),
+            pltpu.VMEM((2, Q, pairs, LANES), f32),
+            pltpu.VMEM((2 * pairs, HALF, LANES), f32),
+            pltpu.VMEM((2 * pairs, HALF, LANES), f32),
+            pltpu.VMEM((Q, LANES), f32),
+            pltpu.VMEM((Q, LANES), f32),
+            dma((chunks,)), dma, dma, dma, dma, dma,
+        ],
+        compiler_params=pltpu.CompilerParams(
+            collective_id=0, has_side_effects=True, vmem_limit_bytes=48 * 1024 * 1024
+        ),
+    )(
+        field.reshape(own, 2 * Q, field.shape[1]),
+        jnp.asarray(first_matrix()),
+        jnp.asarray(second_matrices(groups)),
+    )
+    far = both[1, ::-1]
+    result = jnp.concatenate([both[0], far[:, HALF - 1 :], far[:, : HALF - 1]], axis=1)
+    return result.reshape(block * P_SIZE, LANES)
+
+
+def fits(mesh):
+    groups, planes = mesh.shape["gx"], mesh.shape["gy"]
+    pairs = HALF // groups
+    return pairs % 8 == 0 and (P_SIZE * Q) % (groups * planes * 2 * Q) == 0
+
+
 def solution(mesh):
     in_specs = (P(("gx", "gy"), None),)
     out_specs = P("gx", "gy")
-    return jax.shard_map(body, mesh=mesh, in_specs=in_specs, out_specs=out_specs, check_vma=False)
+    def run(field):
+        fused = fits(mesh) and field.shape[1] == LANES * mesh.shape["gy"]
+        chosen = fused_body if fused else body
+        return jax.shard_map(
+            chosen, mesh=mesh, in_specs=in_specs, out_specs=out_specs, check_vma=False
+        )(field)
+    return run

time: 386 us -> 173 us (0.45); the launches traced: 380 us -> 172 us
  blocking collectives: 208 us -> 0 us
  Pallas kernels: 0 us -> 167 us
  waiting for transfers between devices: 51.2 us -> 0 us
  matrix products: 50 us -> 0 us
  local copies, waits for them, and re-layouts: 45.8 us -> 2.7 us
  starting transfers between devices: 18.9 us -> 0 us
    all_to_all x3 -> x0, blocking collectives: 208 us -> none  [the longest x1 99.3 us: body(): lax.all_to_all(field, 'gy', split_axis=1, concat_axis=0, tiled=True)]
    pallas_call x0 -> x1, Pallas kernels: none -> 167 us  [fused_body(): pl.pallas_call(functools.partial(kernel, groups, planes), out_shape=jax.S...]
    all_to_all x3 -> x0, waiting for transfers between devices: 51.2 us -> none  [the longest x1 28.1 us: body(): lax.all_to_all(turned_real, 'gx', split_axis=0, concat_axis=1, tiled=True)]
    dot_general x8 -> x0, matrix products: 50 us -> none  [the longest x4 24.7 us: mat_dot(): jnp.dot(left, right, precision=highest, preferred_element_type=jnp.float32)]
    all_to_all x3 -> x0, starting transfers between devices: 18.9 us -> none  [the longest x1 8.22 us: body(): lax.all_to_all(odd_rows, 'gx', split_axis=1, concat_axis=0, tiled=True)]
    all_to_all x6 -> x0, local copies, waits for them, and re-layouts: 16.6 us -> none  [the longest x1 5.33 us: body(): lax.all_to_all(field, 'gy', split_axis=1, concat_axis=0, tiled=True)]
    slice x1, local copies, waits for them, and re-layouts: 7.67 us -> 0.02 us  [fused_body(): far[:, HALF - 1:]]
    unnamed x11 -> x4, local copies, waits for them, and re-layouts: 8.93 us -> 2.17 us
  transfers between devices with their start and end apart: 3 -> 0, of which waited for: 3 -> 0; matrix products, arithmetic and copies ran while one was open for 11% -> 0% of each run, Pallas kernels for 0% -> 0%
where the time goes in v1:
time: 173 us; the launch traced here: 172 us
  Pallas kernels  167 us (97%)
  local copies, waits for them, and re-layouts  2.7 us (2%)
  other arithmetic  2.55 us (1%)
    pallas_call x1, Pallas kernels, fused_body(): pl.pallas_call(functools.partial(kernel, groups, planes), out_shape=jax.S...  167 us

profile of v1, /device:TPU:1, one launch (start us, length us, event | category | flops | bytes accessed | tf_op | source)
XLA Modules:
  0.0 172.4 jit_solution(1534155737215031671)
XLA Ops:
  0.0 0.0 copy-start
  0.0 1.2 copy-done
  1.2 0.0 copy-start.1
  1.2 0.9 copy-done.1
  2.2 167.1 %shard_map.37 = f32[2,32,128,128]{3,2,1,0:T(8,128)S(1)} custom-call(f32[4,512,512]{2,1,0:T(8,128)} %bitcast.8, bf16[2,256,256]{2,1,0:T(8,128)(2,1)S(1)} %copy-done.1, bf16[2,2,512,256]{3,2,1,0:T(8,128)(2,1)S(1)} %copy-done), custom_call_target="tpu_custom_call" | custom-call | tf_op jit(solution)/shard_map/pallas_call | solution.py:341
  169.3 0.4 slice_bitcast_fusion
  169.7 0.1 reverse_bitcast_fusion
  169.8 2.6 %pad_maximum_fusion = f32[32,256,128]{2,1,0:T(8,128)} fusion(f32[32,127,128]{2,1,0:T(8,128)S(1)} %bitcast.7, f32[32,1,128]{2,1,0:T(1,128)S(1)} %slice.16, f32[32,128,128]{2,1,0:T(8,128)S(1)} %get-tuple-element.5), kind=kLoop, calls=%fused_computation | loop fusion | flops 2097152 | bytes 8388608 | tf_op jit(solution)/shard_map/concatenate | solution.py:366
  (1 shorter events, 0.0 us)
Async XLA Ops:
  0.0 1.2 copy-start
  1.2 0.9 copy-start.1

commit v2 on v1

--- a/solution.py
+++ b/solution.py
@@ -14,6 +14,7 @@
 HALF = P_SIZE // 2
 LANES = 128
 STEP = 4
+EIGHT = 8
 
 MESH = pl.DeviceIdType.MESH
 highest = lax.Precision.HIGHEST
@@ -148,23 +149,28 @@
 
 
 def kernel(
-    groups, planes, x_ref, first_ref, second_ref, out_ref,
+    groups, planes, x_ref, first_hbm, second_hbm, out_ref, first_ref, second_ref,
     got_rows, part, got_part, coef, turn_cos, turn_sin, end_cos, end_sin,
-    recv_rows, send_rows, recv_part, send_part, recv_coef, send_coef,
+    recv_rows, send_rows, recv_part, send_part, recv_coef, send_coef, recv_tables,
 ):
     gx, gy = lax.axis_index("gx"), lax.axis_index("gy")
     devices = groups * planes
     length = P_SIZE * Q
     pairs = HALF // groups
     chunks = pairs // STEP
+    halves = pairs // EIGHT
     own = x_ref.shape[0]
     width = 2 * STEP
     block = Q // groups
 
+    tables = [
+        pltpu.make_async_copy(first_hbm, first_ref, recv_tables.at[0]),
+        pltpu.make_async_copy(second_hbm, second_ref, recv_tables.at[1]),
+    ]
     barrier = pltpu.get_barrier_semaphore()
 
     def target(offset):
-        return lax.rem(gx + offset // planes, groups), lax.rem(gy + offset % planes, planes)
+        return jnp.bitwise_xor(gx, offset // planes), jnp.bitwise_xor(gy, offset % planes)
 
     def greet(offset, carry):
         pl.semaphore_signal(barrier, inc=1, device_id=target(offset), device_id_type=MESH)
@@ -202,6 +208,8 @@
         return carry
 
     lax.fori_loop(0, chunks, send_chunk, 0)
+    for table in tables:
+        table.start()
 
     slot_row = lax.broadcasted_iota(jnp.int32, (HALF, LANES), 0)
 
@@ -220,6 +228,9 @@
     factor = math.sqrt(2.0 / length)
     end_cos[...] = factor * jnp.cos(end_angle)
     end_sin[...] = factor * jnp.sin(end_angle)
+
+    for table in tables:
+        table.wait()
 
     def first_stage(chunk, carry):
         rows = got_rows.at[chunk]
@@ -247,29 +258,33 @@
                 sin = turn_sin[chunk * width + inner]
                 turned = real * cos + imag * sin, imag * cos - real * sin
                 for plane in range(2):
-                    part[chunk, :, inner, plane] = turned[plane].reshape(groups, pairs, LANES)
-
-        pltpu.make_async_copy(part.at[chunk, gx], got_part.at[gx, chunk], recv_part).start()
-        for offset in range(1, groups):
-            other = lax.rem(gx + offset, groups)
-            pltpu.make_async_remote_copy(
-                src_ref=part.at[chunk, other], dst_ref=got_part.at[gx, chunk],
-                send_sem=send_part, recv_sem=recv_part,
-                device_id=(other, gy), device_id_type=MESH,
+                    parted = turned[plane].reshape(groups, halves, EIGHT, LANES)
+                    for half in range(halves):
+                        part[chunk, half, :, inner, plane] = parted[:, half]
+
+        for half in range(halves):
+            pltpu.make_async_copy(
+                part.at[chunk, half, gx], got_part.at[half, gx, chunk], recv_part.at[half]
             ).start()
+            for offset in range(1, groups):
+                other = jnp.bitwise_xor(gx, offset)
+                pltpu.make_async_remote_copy(
+                    src_ref=part.at[chunk, half, other], dst_ref=got_part.at[half, gx, chunk],
+                    send_sem=send_part, recv_sem=recv_part.at[half],
+                    device_id=(other, gy), device_id_type=MESH,
+                ).start()
         return carry
 
     lax.fori_loop(0, chunks, first_stage, 0)
-    pltpu.make_async_copy(got_part, got_part, recv_part).wait()
-
-    flat_part = got_part.reshape(Q * 2 * pairs, LANES)
+
     flat_coef = coef.reshape(2 * Q * pairs, LANES)
-    eight = 8
-
-    def second_stage(slot, carry):
+
+    def second_stage(half, within, carry):
+        slot = half * EIGHT + within
+        flat_part = got_part.at[half].reshape(Q * 2 * EIGHT, LANES)
         value = jnp.concatenate(
             [
-                flat_part[pl.ds(plane * pairs + slot, Q, stride=2 * pairs), :]
+                flat_part[pl.ds(plane * EIGHT + within, Q, stride=2 * EIGHT), :]
                 for plane in range(2)
             ],
             axis=1,
@@ -295,24 +310,26 @@
         return carry
 
     def coef_copies(step, other):
-        near = step * eight
-        far = pairs - eight - near
+        near = step * EIGHT
+        far = pairs - EIGHT - near
         yield (
-            coef.at[0, pl.ds(pl.multiple_of(other * block, block), block), pl.ds(near, eight)],
-            out_ref.at[0, :, pl.ds(pl.multiple_of(gx * pairs + near, eight), eight)],
+            coef.at[0, pl.ds(pl.multiple_of(other * block, block), block), pl.ds(near, EIGHT)],
+            out_ref.at[0, :, pl.ds(pl.multiple_of(gx * pairs + near, EIGHT), EIGHT)],
         )
         away = groups - 1 - other
         yield (
-            coef.at[1, pl.ds(pl.multiple_of(away * block, block), block), pl.ds(far, eight)],
-            out_ref.at[1, :, pl.ds(pl.multiple_of((groups - 1 - gx) * pairs + far, eight), eight)],
+            coef.at[1, pl.ds(pl.multiple_of(away * block, block), block), pl.ds(far, EIGHT)],
+            out_ref.at[1, :, pl.ds(pl.multiple_of((groups - 1 - gx) * pairs + far, EIGHT), EIGHT)],
         )
 
-    for step in range(pairs // eight):
-        lax.fori_loop(step * eight, (step + 1) * eight, second_stage, 0)
+    for step in range(halves):
+        arrived = got_part.at[step]
+        pltpu.make_async_copy(arrived, arrived, recv_part.at[step]).wait()
+        lax.fori_loop(0, EIGHT, functools.partial(second_stage, step), 0)
         for source, place in coef_copies(step, gx):
             pltpu.make_async_copy(source, place, recv_coef).start()
         for offset in range(1, groups):
-            other = lax.rem(gx + offset, groups)
+            other = jnp.bitwise_xor(gx, offset)
             for source, place in coef_copies(step, other):
                 pltpu.make_async_remote_copy(
                     src_ref=source, dst_ref=place, send_sem=send_coef, recv_sem=recv_coef,
@@ -322,7 +339,7 @@
     pltpu.make_async_copy(out_ref, out_ref, recv_coef).wait()
     sent = x_ref.at[:, pl.ds(0, 2 * Q - 2 * Q // devices), :]
     pltpu.make_async_copy(sent, sent, send_rows).wait()
-    sent = part.at[:, pl.ds(0, groups - 1)]
+    sent = part.at[:, :, pl.ds(0, groups - 1)]
     pltpu.make_async_copy(sent, sent, send_part).wait()
     sent = coef.at[:, pl.ds(0, Q - block)]
     pltpu.make_async_copy(sent, sent, send_coef).wait()
@@ -332,27 +349,32 @@
     groups, planes = lax.axis_size("gx"), lax.axis_size("gy")
     pairs = HALF // groups
     chunks = pairs // STEP
+    halves = pairs // EIGHT
     block = Q // groups
     own = field.shape[0] // (2 * Q)
     width = 2 * STEP
     f32 = jnp.float32
     vmem = pl.BlockSpec(memory_space=pltpu.VMEM)
+    hbm = pl.BlockSpec(memory_space=pltpu.HBM)
+    bf16 = jnp.bfloat16
     dma = pltpu.SemaphoreType.DMA
     both = pl.pallas_call(
         functools.partial(kernel, groups, planes),
         out_shape=jax.ShapeDtypeStruct((2, block, HALF, LANES), f32),
-        in_specs=[pl.BlockSpec(memory_space=pl.ANY), vmem, vmem],
+        in_specs=[pl.BlockSpec(memory_space=pl.ANY), hbm, hbm],
         out_specs=vmem,
         scratch_shapes=[
+            pltpu.VMEM((2, P_SIZE, P_SIZE), bf16),
+            pltpu.VMEM((2, 2, 2 * Q, Q), bf16),
             pltpu.VMEM((chunks, HALF, 2 * width, LANES), f32),
-            pltpu.VMEM((chunks, groups, width, 2, pairs, LANES), f32),
-            pltpu.VMEM((groups, chunks, width, 2, pairs, LANES), f32),
+            pltpu.VMEM((chunks, halves, groups, width, 2, EIGHT, LANES), f32),
+            pltpu.VMEM((halves, groups, chunks, width, 2, EIGHT, LANES), f32),
             pltpu.VMEM((2, Q, pairs, LANES), f32),
             pltpu.VMEM((2 * pairs, HALF, LANES), f32),
             pltpu.VMEM((2 * pairs, HALF, LANES), f32),
             pltpu.VMEM((Q, LANES), f32),
             pltpu.VMEM((Q, LANES), f32),
-            dma((chunks,)), dma, dma, dma, dma, dma,
+            dma((chunks,)), dma, dma((halves,)), dma, dma, dma, dma((2,)),
         ],
         compiler_params=pltpu.CompilerParams(
             collective_id=0, has_side_effects=True, vmem_limit_bytes=48 * 1024 * 1024
@@ -370,7 +392,8 @@
 def fits(mesh):
     groups, planes = mesh.shape["gx"], mesh.shape["gy"]
     pairs = HALF // groups
-    return pairs % 8 == 0 and (P_SIZE * Q) % (groups * planes * 2 * Q) == 0
+    powers = groups & (groups - 1) == 0 and planes & (planes - 1) == 0
+    return powers and pairs % 8 == 0 and (P_SIZE * Q) % (groups * planes * 2 * Q) == 0
 
 
 def solution(mesh):

time: 173 us -> 167 us (0.965)
  Pallas kernels: 167 us -> 161 us
    pallas_call x1, Pallas kernels: 167 us -> 161 us  [fused_body(): pl.pallas_call(functools.partial(kernel, groups, planes), out_shape=jax.S...]
where the time goes in v2:
time: 167 us
  Pallas kernels  161 us (96%)
  local copies, waits for them, and re-layouts  2.7 us (2%)
  other arithmetic  2.55 us (2%)
    pallas_call x1, Pallas kernels, fused_body(): pl.pallas_call(functools.partial(kernel, groups, planes), out_shape=jax.S...  161 us

profile of v2, /device:TPU:1, one launch (start us, length us, event | category | flops | bytes accessed | tf_op | source)
XLA Modules:
  0.0 166.6 jit_solution(15613645565127630568)
XLA Ops:
  0.0 0.0 copy-start
  0.0 1.2 copy-done
  1.2 0.0 copy-start.1
  1.2 0.9 copy-done.1
  2.2 161.3 %shard_map.37 = f32[2,32,128,128]{3,2,1,0:T(8,128)S(1)} custom-call(f32[4,512,512]{2,1,0:T(8,128)} %bitcast.8, bf16[2,256,256]{2,1,0:T(8,128)(2,1)S(1)} %copy-done.1, bf16[2,2,512,256]{3,2,1,0:T(8,128)(2,1)S(1)} %copy-done), custom_call_target="tpu_custom_call" | custom-call | tf_op jit(solution)/shard_map/pallas_call | solution.py:361
  163.5 0.4 slice_bitcast_fusion
  163.9 0.1 reverse_bitcast_fusion
  164.1 2.6 %pad_maximum_fusion = f32[32,256,128]{2,1,0:T(8,128)} fusion(f32[32,127,128]{2,1,0:T(8,128)S(1)} %bitcast.7, f32[32,1,128]{2,1,0:T(1,128)S(1)} %slice.16, f32[32,128,128]{2,1,0:T(8,128)S(1)} %get-tuple-element.5), kind=kLoop, calls=%fused_computation | loop fusion | flops 2097152 | bytes 8388608 | tf_op jit(solution)/shard_map/concatenate | solution.py:388
  (1 shorter events, 0.0 us)
Async XLA Ops:
  0.0 1.2 copy-start
  1.2 0.9 copy-start.1

commit v3 on v2

--- a/solution.py
+++ b/solution.py
@@ -3,7 +3,6 @@
 
 import jax
 import jax.numpy as jnp
-import numpy as np
 from jax import lax
 from jax.experimental import pallas as pl
 from jax.experimental.pallas import tpu as pltpu
@@ -98,44 +97,6 @@
     return arrived.reshape(local_q * P_SIZE, col_width)
 
 
-def split_np(table):
-    high = table.astype(jnp.bfloat16)
-    low = (table - high.astype(np.float64)).astype(jnp.bfloat16)
-    return np.stack([high, low])
-
-
-def order_of_q(groups):
-    pairs = HALF // groups
-    order = []
-    for group in range(groups):
-        for start in range(0, pairs, STEP):
-            low = [group * pairs + start + i for i in range(STEP)]
-            order += low + [Q - 1 - q for q in low]
-    return np.array(order)
-
-
-def first_matrix():
-    low = np.arange(HALF)
-    place = np.concatenate([low, P_SIZE - 1 - low])
-    angle = 2 * np.pi / P_SIZE * (low[:, None] * place[None, :] % P_SIZE)
-    real, imag = np.cos(angle), -np.sin(angle)
-    imag[0] = np.cos(np.pi * place)
-    return split_np(np.concatenate([real, imag]))
-
-
-def second_matrices(groups):
-    length = P_SIZE * Q
-    q = order_of_q(groups)[None, :]
-    k2 = np.arange(Q)[:, None]
-    angle = 2 * np.pi / Q * (k2 * q % Q)
-    usual = np.concatenate([np.cos(angle), np.sin(angle)])
-    factor = math.sqrt(2.0 / length)
-    def row(k):
-        return factor * np.cos(2 * np.pi / (4 * length) * (k * (4 * q + 1) % (4 * length)))
-    special = np.concatenate([row(P_SIZE * k2), row(HALF + P_SIZE * (Q - 1 - k2))])
-    return np.stack([split_np(usual), split_np(special)])
-
-
 def split(value):
     high = value.astype(jnp.bfloat16)
     low = (value - high.astype(jnp.float32)).astype(jnp.bfloat16)
@@ -149,9 +110,9 @@
 
 
 def kernel(
-    groups, planes, x_ref, first_hbm, second_hbm, out_ref, first_ref, second_ref,
+    groups, planes, x_ref, out_ref, first_ref, second_ref,
     got_rows, part, got_part, coef, turn_cos, turn_sin, end_cos, end_sin,
-    recv_rows, send_rows, recv_part, send_part, recv_coef, send_coef, recv_tables,
+    recv_rows, send_rows, recv_part, send_part, recv_coef, send_coef,
 ):
     gx, gy = lax.axis_index("gx"), lax.axis_index("gy")
     devices = groups * planes
@@ -163,10 +124,6 @@
     width = 2 * STEP
     block = Q // groups
 
-    tables = [
-        pltpu.make_async_copy(first_hbm, first_ref, recv_tables.at[0]),
-        pltpu.make_async_copy(second_hbm, second_ref, recv_tables.at[1]),
-    ]
     barrier = pltpu.get_barrier_semaphore()
 
     def target(offset):
@@ -208,8 +165,38 @@
         return carry
 
     lax.fori_loop(0, chunks, send_chunk, 0)
-    for table in tables:
-        table.start()
+
+    def iota(rows, columns, dimension):
+        return lax.broadcasted_iota(jnp.int32, (rows, columns), dimension)
+
+    def angles(steps, period):
+        return (steps & (period - 1)).astype(jnp.float32) * (2 * math.pi / period)
+
+    frequency_row, column = iota(HALF, P_SIZE, 0), iota(HALF, P_SIZE, 1)
+    place = jnp.where(column < HALF, column, P_SIZE - 1 - (column - HALF))
+    angle = angles(frequency_row * place, P_SIZE)
+    middle = 1.0 - 2.0 * (place & 1).astype(jnp.float32)
+    first_real, first_imag = jnp.cos(angle), jnp.where(frequency_row == 0, middle, -jnp.sin(angle))
+    first_ref[0, :HALF], first_ref[1, :HALF] = split(first_real)
+    first_ref[0, HALF:], first_ref[1, HALF:] = split(first_imag)
+
+    k2, index = iota(Q, Q, 0), iota(Q, Q, 1)
+    inner = index & (width - 1)
+    base = (index >> (width.bit_length() - 1)) * STEP
+    q = jnp.where(inner < STEP, base + inner, Q - 1 - (base + inner - STEP))
+    angle = angles(k2 * q, Q)
+    amplitude = math.sqrt(2.0 / length)
+    for which, half, table in (
+        (0, 0, jnp.cos(angle)),
+        (0, 1, jnp.sin(angle)),
+        (1, 0, amplitude * jnp.cos(angles(P_SIZE * k2 * (4 * q + 1), 4 * length))),
+        (1, 1, amplitude * jnp.cos(
+            angles((HALF + P_SIZE * (Q - 1 - k2)) * (4 * q + 1), 4 * length)
+        )),
+    ):
+        high, low = split(table)
+        second_ref[which, 0, half * Q : (half + 1) * Q] = high
+        second_ref[which, 1, half * Q : (half + 1) * Q] = low
 
     slot_row = lax.broadcasted_iota(jnp.int32, (HALF, LANES), 0)
 
@@ -228,9 +215,6 @@
     factor = math.sqrt(2.0 / length)
     end_cos[...] = factor * jnp.cos(end_angle)
     end_sin[...] = factor * jnp.sin(end_angle)
-
-    for table in tables:
-        table.wait()
 
     def first_stage(chunk, carry):
         rows = got_rows.at[chunk]
@@ -355,13 +339,12 @@
     width = 2 * STEP
     f32 = jnp.float32
     vmem = pl.BlockSpec(memory_space=pltpu.VMEM)
-    hbm = pl.BlockSpec(memory_space=pltpu.HBM)
     bf16 = jnp.bfloat16
     dma = pltpu.SemaphoreType.DMA
     both = pl.pallas_call(
         functools.partial(kernel, groups, planes),
         out_shape=jax.ShapeDtypeStruct((2, block, HALF, LANES), f32),
-        in_specs=[pl.BlockSpec(memory_space=pl.ANY), hbm, hbm],
+        in_specs=[pl.BlockSpec(memory_space=pl.ANY)],
         out_specs=vmem,
         scratch_shapes=[
             pltpu.VMEM((2, P_SIZE, P_SIZE), bf16),
@@ -374,16 +357,12 @@
             pltpu.VMEM((2 * pairs, HALF, LANES), f32),
             pltpu.VMEM((Q, LANES), f32),
             pltpu.VMEM((Q, LANES), f32),
-            dma((chunks,)), dma, dma((halves,)), dma, dma, dma, dma((2,)),
+            dma((chunks,)), dma, dma((halves,)), dma, dma, dma,
         ],
         compiler_params=pltpu.CompilerParams(
             collective_id=0, has_side_effects=True, vmem_limit_bytes=48 * 1024 * 1024
         ),
-    )(
-        field.reshape(own, 2 * Q, field.shape[1]),
-        jnp.asarray(first_matrix()),
-        jnp.asarray(second_matrices(groups)),
-    )
+    )(field.reshape(own, 2 * Q, field.shape[1]))
     far = both[1, ::-1]
     result = jnp.concatenate([both[0], far[:, HALF - 1 :], far[:, : HALF - 1]], axis=1)
     return result.reshape(block * P_SIZE, LANES)

time: 167 us -> 165 us (0.988)
  local copies, waits for them, and re-layouts: 2.7 us -> 0.53 us
    unnamed x4 -> x0, local copies, waits for them, and re-layouts: 2.17 us -> none
where the time goes in v3:
time: 165 us
  Pallas kernels  161 us (98%)
  other arithmetic  2.55 us (2%)
    pallas_call x1, Pallas kernels, fused_body(): pl.pallas_call(functools.partial(kernel, groups, planes), out_shape=jax.S...  161 us

profile of v3, /device:TPU:1, one launch (start us, length us, event | category | flops | bytes accessed | tf_op | source)
XLA Modules:
  0.0 164.5 jit_solution(5086513996568598615)
XLA Ops:
  0.0 161.4 %shard_map.17 = f32[2,32,128,128]{3,2,1,0:T(8,128)S(1)} custom-call(f32[4,512,512]{2,1,0:T(8,128)} %bitcast.8), custom_call_target="tpu_custom_call" | custom-call | tf_op jit(solution)/shard_map/pallas_call | solution.py:344
  161.4 0.4 slice_bitcast_fusion
  161.8 0.1 reverse_bitcast_fusion
  162.0 2.6 %pad_maximum_fusion = f32[32,256,128]{2,1,0:T(8,128)} fusion(f32[32,127,128]{2,1,0:T(8,128)S(1)} %bitcast.7, f32[32,1,128]{2,1,0:T(1,128)S(1)} %slice.16, f32[32,128,128]{2,1,0:T(8,128)S(1)} %get-tuple-element.5), kind=kLoop, calls=%fused_computation | loop fusion | flops 2097152 | bytes 8388608 | tf_op jit(solution)/shard_map/concatenate | solution.py:367
  (1 shorter events, 0.0 us)

commit v4 on v3

--- a/solution.py
+++ b/solution.py
@@ -250,7 +250,7 @@
             pltpu.make_async_copy(
                 part.at[chunk, half, gx], got_part.at[half, gx, chunk], recv_part.at[half]
             ).start()
-            for offset in range(1, groups):
+            for offset in (*range(2, groups, 2), *range(1, groups, 2)[1:], 1):
                 other = jnp.bitwise_xor(gx, offset)
                 pltpu.make_async_remote_copy(
                     src_ref=part.at[chunk, half, other], dst_ref=got_part.at[half, gx, chunk],
@@ -312,7 +312,7 @@
         lax.fori_loop(0, EIGHT, functools.partial(second_stage, step), 0)
         for source, place in coef_copies(step, gx):
             pltpu.make_async_copy(source, place, recv_coef).start()
-        for offset in range(1, groups):
+        for offset in (*range(2, groups, 2), *range(1, groups, 2)[1:], 1):
             other = jnp.bitwise_xor(gx, offset)
             for source, place in coef_copies(step, other):
                 pltpu.make_async_remote_copy(

time: 165 us -> 165 us (level)
  no operation moved by 1% of the time
where the time goes in v4:
time: 165 us; the launch traced here: 164 us
  Pallas kernels  161 us (98%)
  other arithmetic  2.55 us (2%)
    pallas_call x1, Pallas kernels, fused_body(): pl.pallas_call(functools.partial(kernel, groups, planes), out_shape=jax.S...  161 us

profile of v4, /device:TPU:1, one launch (start us, length us, event | category | flops | bytes accessed | tf_op | source)
XLA Modules:
  0.0 164.3 jit_solution(10942148604109701387)
XLA Ops:
  0.0 161.2 %shard_map.17 = f32[2,32,128,128]{3,2,1,0:T(8,128)S(1)} custom-call(f32[4,512,512]{2,1,0:T(8,128)} %bitcast.8), custom_call_target="tpu_custom_call" | custom-call | tf_op jit(solution)/shard_map/pallas_call | solution.py:344
  161.2 0.4 slice_bitcast_fusion
  161.6 0.1 reverse_bitcast_fusion
  161.7 2.6 %pad_maximum_fusion = f32[32,256,128]{2,1,0:T(8,128)} fusion(f32[32,127,128]{2,1,0:T(8,128)S(1)} %bitcast.7, f32[32,1,128]{2,1,0:T(1,128)S(1)} %slice.16, f32[32,128,128]{2,1,0:T(8,128)S(1)} %get-tuple-element.5), kind=kLoop, calls=%fused_computation | loop fusion | flops 2097152 | bytes 8388608 | tf_op jit(solution)/shard_map/concatenate | solution.py:367
  (1 shorter events, 0.0 us)
